TPU v7x, 32 devices: a whole 2x2x4 slice. The times are simulated.
32 devices in a mesh: ep: 4 (over z), fsdp: 8 (over y, x, core).
Axes of the slice: x: 2, y: 2, z: 4, core: 2. Of those that a mesh axis runs over, the one named last changes fastest.
Arguments:
- train_gate: float32 [64, 2048, 1408], P('ep', 'fsdp'), may hold values from -0.1875 to 0.1875
- train_up: float32 [64, 2048, 1408], P('ep', 'fsdp'), may hold values from -0.1875 to 0.1875
- train_down: float32 [64, 1408, 2048], P('ep', None, 'fsdp'), may hold values from -0.21875 to 0.21875
- router_weight: float32 [2048, 64], P('fsdp', 'ep'), may hold values from -0.125 to 0.125
- router_gain: float32 [2048], P('fsdp'), may hold values from 0.25 to 1.75
Outputs:
- ready_gate: bfloat16 [64, 2048, 1408], P('ep', None, 'fsdp')
- ready_up: bfloat16 [64, 2048, 1408], P('ep', None, 'fsdp')
- ready_down: bfloat16 [64, 1408, 2048], P('ep', 'fsdp')
- scale_gate: float32 [64, 1408], P('ep', 'fsdp')
- scale_up: float32 [64, 1408], P('ep', 'fsdp')
- scale_down: float32 [64, 1408], P('ep', 'fsdp')
- serve_router: bfloat16 [2048, 64], replicated
All inputs are finite; a program needn't handle non-finite values. Where the computation divides by a largest or mean magnitude, that divisor is 1e-20 or more.
Results may differ from a plain program's by a relative error of at most 0.012.
Values may be sent and summed in bfloat16 or wider, within the bound.
A program may use at most 192 MiB of HBM per device.

v0:
```python
import jax
import jax.numpy as jnp
from jax import lax
from jax.sharding import PartitionSpec as P

D_MODEL = 2048


def shards(train_gate, train_up, train_down, router_weight, router_gain):
    total_gate, total_up, total_down = (
        lax.psum(jnp.sum(jnp.abs(train_gate), axis=1).astype(jnp.bfloat16), "fsdp").astype(
            jnp.float32
        ),
        lax.psum(jnp.sum(jnp.abs(train_up), axis=1).astype(jnp.bfloat16), "fsdp").astype(
            jnp.float32
        ),
        lax.psum(jnp.sum(jnp.abs(train_down), axis=2).astype(jnp.bfloat16), "fsdp").astype(
            jnp.float32
        ),
    )
    scale_gate = total_gate / D_MODEL
    scale_up = total_up / D_MODEL
    scale_down = total_down / D_MODEL
    narrow_gate, narrow_up, narrow_down = (
        (train_gate / jnp.expand_dims(scale_gate, 1)).astype(jnp.bfloat16),
        (train_up / jnp.expand_dims(scale_up, 1)).astype(jnp.bfloat16),
        (train_down / jnp.expand_dims(scale_down, 2)).astype(jnp.bfloat16),
    )
    ready_gate, ready_up = (
        lax.all_to_all(narrow_gate, "fsdp", split_axis=2, concat_axis=1, tiled=True),
        lax.all_to_all(narrow_up, "fsdp", split_axis=2, concat_axis=1, tiled=True),
    )
    ready_down = lax.all_to_all(narrow_down, "fsdp", split_axis=1, concat_axis=2, tiled=True)
    scale_gate = lax.dynamic_slice_in_dim(
        scale_gate, lax.axis_index("fsdp") * ready_gate.shape[2], ready_gate.shape[2], axis=1
    )
    scale_up = lax.dynamic_slice_in_dim(
        scale_up, lax.axis_index("fsdp") * ready_up.shape[2], ready_up.shape[2], axis=1
    )
    scale_down = lax.dynamic_slice_in_dim(
        scale_down, lax.axis_index("fsdp") * ready_down.shape[1], ready_down.shape[1], axis=1
    )
    part_router = (router_weight * router_gain[:, None]).astype(jnp.bfloat16)
    row_router = lax.all_gather(part_router, "fsdp", axis=0, tiled=True)
    serve_router = lax.all_gather(row_router, "ep", axis=1, tiled=True)
    return (ready_gate, ready_up, ready_down, scale_gate, scale_up, scale_down, serve_router)


def solution(mesh):
    in_specs = (
        P("ep", "fsdp", None),
        P("ep", "fsdp", None),
        P("ep", None, "fsdp"),
        P("fsdp", "ep"),
        P("fsdp"),
    )
    out_specs = (
        P("ep", None, "fsdp"),
        P("ep", None, "fsdp"),
        P("ep", "fsdp", None),
        P("ep", "fsdp"),
        P("ep", "fsdp"),
        P("ep", "fsdp"),
        P(),
    )
    return jax.shard_map(shards, mesh=mesh, in_specs=in_specs, out_specs=out_specs, check_vma=False)
```

profile of v0, /device:TPU:0, one launch (start us, length us, event | category | flops | bytes accessed | tf_op | source)
XLA Modules:
  0.0 617.4 jit_solution(11987987628351158617)
XLA Ops:
  7.2 9.2 %abs_reduce_fusion = bf16[16,1408]{1,0:T(8,128)(2,1)} fusion(f32[16,1408,256]{2,1,0:T(8,128)} %param.7), kind=kLoop, calls=%fused_computation.2 | loop fusion | flops 11511808 | bytes 23113728 | tf_op jit(solution)/shard_map/reduce_sum | solution.py:17
  16.4 5.0 copy-done
  21.4 11.7 %abs_reduce_fusion.1 = (bf16[16,1408]{1,0:T(8,128)(2,1)}, bf16[16,1408]{1,0:T(8,128)(2,1)}) fusion(f32[16,256,1408]{2,1,0:T(8,128)S(1)} %copy-done, f32[16,256,1408]{2,1,0:T(8,128)} %param.5), kind=kLoop, calls=%fused_computation.4 | loop fusion | flops 23023616 | bytes 46227456 | tf_op jit(solution)/shard_map/reduce_sum | solution.py:14
  33.1 23.7 %copy.28 = f32[16,256,1408]{1,0,2:T(8,128)} copy(f32[16,256,1408]{2,1,0:T(8,128)} %param.6) | data formatting | bytes 46137344 | tf_op args[1]
  56.8 31.4 %all-reduce.3.cloned.1.call-done = (bf16[16,1408]{1,0:T(8,128)(2,1)}, bf16[16,1408]{1,0:T(8,128)(2,1)}, bf16[16,1408]{1,0:T(8,128)(2,1)}) async-done(((bf16[16,1408]{1,0:T(8,128)(2,1)}, bf16[16,1408]{1,0:T(8,128)(2,1)}, bf16[16,1408]{1,0:T(8,128)(2,1)}), (bf16[16,1408]{1,0:T(8,128)(2,1)}, bf16[16,1408]{1,0:T(8,128)(2,1)}, bf16[16,1408]{1,0:T(8,128)(2,1)})) %all-reduce.3.cloned.1.call-update) | async-done | bytes 135184 | tf_op jit(solution)/shard_map/psum | solution.py:11
  88.3 0.8 convert_multiply_fusion.1
  89.3 14.2 %divide_convert_fusion = bf16[16,256,1408]{1,0,2:T(8,128)(2,1)} fusion(f32[16,256,1408]{1,0,2:T(8,128)} %copy.28, f32[16,1408]{0,1:T(8,128)S(1)} %copy.27), kind=kLoop, calls=%fused_computation.3 | loop fusion | flops 11534336 | bytes 34693120 | tf_op jit(solution)/shard_map/convert_element_type | solution.py:26
  103.5 5.2 all-to-all-start.1
  108.8 23.7 %copy.24 = f32[16,256,1408]{1,0,2:T(8,128)} copy(f32[16,256,1408]{2,1,0:T(8,128)} %param.5) | data formatting | bytes 46137344 | tf_op args[0]
  132.8 14.2 %divide_convert_fusion.1 = bf16[16,256,1408]{1,0,2:T(8,128)(2,1)} fusion(f32[16,256,1408]{1,0,2:T(8,128)} %copy.24, f32[16,1408]{0,1:T(8,128)S(1)} %copy.23), kind=kLoop, calls=%fused_computation.5 | loop fusion | flops 11534336 | bytes 34693120 | tf_op jit(solution)/shard_map/convert_element_type | solution.py:25
  147.0 89.5 %all-to-all-done.1 = bf16[16,256,1408]{1,0,2:T(8,128)(2,1)} async-done(((bf16[16,256,1408]{1,0,2:T(8,128)(2,1)}), bf16[16,256,1408]{1,0,2:T(8,128)(2,1)}, u32[]{:S(2)}, u32[]{:S(2)}) %all-to-all-start.1) | async-done | bytes 11534368 | tf_op jit(solution)/shard_map/all_to_all | solution.py:31
  236.5 5.3 all-to-all-start
  242.1 32.6 %fusion = bf16[16,1408,256]{2,0,1:T(8,128)(2,1)} fusion(f32[16,1408,256]{2,1,0:T(8,128)} %param.7, f32[16,1408]{0,1:T(8,128)S(1)} %copy.31), kind=kLoop, calls=%fused_computation.1 | loop fusion | flops 11534336 | bytes 34693120 | tf_op jit(solution)/shard_map/convert_element_type | solution.py:27
  274.7 94.8 %all-to-all-done = bf16[16,256,1408]{1,0,2:T(8,128)(2,1)} async-done(((bf16[16,256,1408]{1,0,2:T(8,128)(2,1)}), bf16[16,256,1408]{1,0,2:T(8,128)(2,1)}, u32[]{:S(2)}, u32[]{:S(2)}) %all-to-all-start) | async-done | bytes 11534368 | tf_op jit(solution)/shard_map/all_to_all | solution.py:30
  369.6 5.3 all-to-all-start.2
  374.9 130.9 %all_gather.6 = bf16[2048,16]{0,1:T(8,128)(2,1)S(1)} all-gather(bf16[256,16]{0,1:T(8,128)(2,1)S(1)} %multiply_convert_fusion), channel_id=1, replica_groups=mesh['ep'=4,'fsdp'=8] {'fsdp'}, dimensions={0}, use_global_device_ids=true | all-gather | bytes 73728 | tf_op jit(solution)/shard_map/all_gather | solution.py:44
  505.8 14.2 %all_gather.7 = bf16[2048,64]{0,1:T(8,128)(2,1)S(1)} all-gather(bf16[2048,16]{0,1:T(8,128)(2,1)S(1)} %all_gather.6), channel_id=1, replica_groups=mesh['ep'=4,'fsdp'=8] {'ep'}, dimensions={1}, use_global_device_ids=true | all-gather | bytes 327680 | tf_op jit(solution)/shard_map/all_gather | solution.py:45
  522.0 11.3 %copy.30 = bf16[16,8,256,176]{2,1,3,0:T(8,128)(2,1)} copy(bf16[16,8,256,176]{2,0,3,1:T(8,128)(2,1)} %bitcast.5) | data formatting | bytes 23068672 | tf_op jit(solution)/shard_map/all_to_all | solution.py:31
  533.3 18.0 %all_to_all.46 = bf16[16,2048,176]{1,2,0:T(8,128)(2,1)} reshape(bf16[16,8,256,176]{2,1,3,0:T(8,128)(2,1)} %copy.30) | data formatting | bytes 23068672 | tf_op jit(solution)/shard_map/all_to_all | solution.py:31
  551.3 11.3 %copy.26 = bf16[16,8,256,176]{2,1,3,0:T(8,128)(2,1)} copy(bf16[16,8,256,176]{2,0,3,1:T(8,128)(2,1)} %bitcast.2) | data formatting | bytes 23068672 | tf_op jit(solution)/shard_map/all_to_all | solution.py:30
  562.6 18.0 %all_to_all.42 = bf16[16,2048,176]{1,2,0:T(8,128)(2,1)} reshape(bf16[16,8,256,176]{2,1,3,0:T(8,128)(2,1)} %copy.26) | data formatting | bytes 23068672 | tf_op jit(solution)/shard_map/all_to_all | solution.py:30
  580.6 11.3 %copy.33 = bf16[16,176,8,256]{3,2,1,0:T(8,128)(2,1)} copy(bf16[16,176,8,256]{3,0,1,2:T(8,128)(2,1)} %bitcast.7) | data formatting | bytes 23068672 | tf_op jit(solution)/shard_map/all_to_all | solution.py:33
  591.9 18.0 %all_to_all.50 = bf16[16,176,2048]{2,1,0:T(8,128)(2,1)} reshape(bf16[16,176,8,256]{3,2,1,0:T(8,128)(2,1)} %copy.33) | data formatting | bytes 23068672 | tf_op jit(solution)/shard_map/all_to_all | solution.py:33
  609.9 0.7 copy.43
  (21 shorter events, 2.9 us)
Async XLA Ops:
  7.2 81.1 %all-reduce.3.cloned.1.call-start = ((), (), s32[]{:S(2)}) async-start(), calls=%async_computation.3 | async-start | bytes 270336 | tf_op jit(solution)/shard_map/psum | solution.py:11
  7.2 14.2 %copy-start = (f32[16,256,1408]{2,1,0:T(8,128)S(1)}, f32[16,256,1408]{2,1,0:T(8,128)}, u32[]{:S(2)}) copy-start(f32[16,256,1408]{2,1,0:T(8,128)} %param.6) | copy-start | bytes 69206016
  103.5 133.0 %all-to-all-start.1 = ((bf16[16,256,1408]{1,0,2:T(8,128)(2,1)}), bf16[16,256,1408]{1,0,2:T(8,128)(2,1)}, u32[]{:S(2)}, u32[]{:S(2)}) async-start(bf16[16,256,1408]{1,0,2:T(8,128)(2,1)} %divide_convert_fusion), calls=%async_computation.1 | async-start | bytes 23068672 | tf_op jit(solution)/shard_map/all_to_all | solution.py:31
  108.8 23.7 %copy-start.2 = (bf16[16,1408]{1,0:T(8,128)(2,1)S(1)}, bf16[16,1408]{1,0:T(8,128)(2,1)}, u32[]{:S(2)}) copy-start(bf16[16,1408]{1,0:T(8,128)(2,1)} %get-tuple-element.7) | copy-start | bytes 135172
  132.8 109.0 %copy-start.1 = (bf16[16,1408]{1,0:T(8,128)(2,1)S(1)}, bf16[16,1408]{1,0:T(8,128)(2,1)}, u32[]{:S(2)}) copy-start(bf16[16,1408]{1,0:T(8,128)(2,1)} %get-tuple-element.9) | copy-start | bytes 135172
  236.5 133.0 %all-to-all-start = ((bf16[16,256,1408]{1,0,2:T(8,128)(2,1)}), bf16[16,256,1408]{1,0,2:T(8,128)(2,1)}, u32[]{:S(2)}, u32[]{:S(2)}) async-start(bf16[16,256,1408]{1,0,2:T(8,128)(2,1)} %divide_convert_fusion.1), calls=%async_computation | async-start | bytes 23068672 | tf_op jit(solution)/shard_map/all_to_all | solution.py:30
  242.1 132.7 %copy-start.3 = (f32[256,16]{0,1:T(8,128)S(1)}, f32[256,16]{0,1:T(8,128)}, u32[]{:S(2)}) copy-start(f32[256,16]{0,1:T(8,128)} %param.8) | copy-start | bytes 49156
  242.1 132.7 %copy-start.4 = (f32[256]{0:T(256)S(1)}, f32[256]{0:T(256)}, u32[]{:S(2)}) copy-start(f32[256]{0:T(256)} %param.9) | copy-start | bytes 3076
  369.6 211.0 %all-to-all-start.2 = ((bf16[16,1408,256]{2,0,1:T(8,128)(2,1)}), bf16[16,1408,256]{2,0,1:T(8,128)(2,1)}, u32[]{:S(2)}, u32[]{:S(2)}) async-start(bf16[16,1408,256]{2,0,1:T(8,128)(2,1)} %fusion), calls=%async_computation.2 | async-start | bytes 23068672 | tf_op jit(solution)/shard_map/all_to_all | solution.py:33
Sparse Core Ops, SparseCore 0:
  33.2 54.9 all-reduce.2
where the time goes:
time: 620 us; the launch traced here: 617 us
  waiting for transfers between devices  216 us (35%)
  blocking collectives  145 us (23%)
  local copies, waits for them, and re-layouts  144 us (23%)
  other arithmetic  82.7 us (13%)
  starting transfers between devices  15.8 us (3%)
  between operations  14.2 us (2%)
    all_gather x1, blocking collectives, shards(): row_router = lax.all_gather(part_router, 'fsdp', axis=0, tiled=True)  131 us
    all_to_all x1, waiting for transfers between devices, shards(): lax.all_to_all(narrow_gate, 'fsdp', split_axis=2, concat_axis=1, tiled=True)  94.8 us
    all_to_all x1, waiting for transfers between devices, shards(): lax.all_to_all(narrow_up, 'fsdp', split_axis=2, concat_axis=1, tiled=True)  89.5 us
    unnamed x13, local copies, waits for them, and re-layouts  53.1 us
    convert_element_type x1, other arithmetic, shards(): (train_down / jnp.expand_dims(scale_down, 2)).astype(jnp.bfloat16)  32.6 us
    psum x1, waiting for transfers between devices, shards(): lax.psum(jnp.sum(jnp.abs(train_gate), axis=1).astype(jnp.bfloat16), 'fsdp')  31.4 us
    all_to_all x2, local copies, waits for them, and re-layouts, shards(): lax.all_to_all(narrow_gate, 'fsdp', split_axis=2, concat_axis=1, tiled=True)  29.3 us
    all_to_all x2, local copies, waits for them, and re-layouts, shards(): lax.all_to_all(narrow_up, 'fsdp', split_axis=2, concat_axis=1, tiled=True)  29.3 us
  transfers between devices with their start and end apart: 4, of which 3 were waited for; matrix products, arithmetic and copies ran while one was open for 19% of the time, Pallas kernels for 0%

commit v1 on v0

--- a/solution.py
+++ b/solution.py
@@ -8,9 +8,10 @@
 
 def shards(train_gate, train_up, train_down, router_weight, router_gain):
     total_gate, total_up, total_down = (
-        lax.psum(jnp.sum(jnp.abs(train_gate), axis=1).astype(jnp.bfloat16), "fsdp").astype(
-            jnp.float32
-        ),
+        jnp.sum(
+            lax.all_gather(jnp.sum(jnp.abs(train_gate), axis=1).astype(jnp.bfloat16), "fsdp"),
+            axis=0,
+        ).astype(jnp.float32),
         lax.psum(jnp.sum(jnp.abs(train_up), axis=1).astype(jnp.bfloat16), "fsdp").astype(
             jnp.float32
         ),

time: 620 us -> 596 us (0.961)
  waiting for transfers between devices: 216 us -> 179 us
  blocking collectives: 145 us -> 156 us
  other arithmetic: 82.7 us -> 90 us
    all_to_all x1, waiting for transfers between devices: 94.8 us -> 0.01 us  [shards(): lax.all_to_all(narrow_gate, 'fsdp', split_axis=2, concat_axis=1, tiled=True)]
    psum x1, waiting for transfers between devices: 31.4 us -> 83.2 us  [shards(): lax.psum(jnp.sum(jnp.abs(train_up), axis=1).astype(jnp.bfloat16), 'fsdp')]
    all_gather x0 -> x1, blocking collectives: none -> 11.1 us  [shards(): lax.all_gather(jnp.sum(jnp.abs(train_gate), axis=1).astype(jnp.bfloat16),...]
    reduce_sum x0 -> x2, other arithmetic: none -> 9.3 us  [the longest x1 9.25 us: shards(): jnp.sum(jnp.abs(train_gate), axis=1).astype(jnp.bfloat16)]
    unnamed x13 -> x9, local copies, waits for them, and re-layouts: 53.1 us -> 48.1 us
  transfers between devices with their start and end apart: 4 -> 4, of which waited for: 3 -> 2; matrix products, arithmetic and copies ran while one was open for 19% -> 19% of each run, Pallas kernels for 0% -> 0%
where the time goes in v1:
time: 596 us; the launch traced here: 593 us
  waiting for transfers between devices  179 us (30%)
  blocking collectives  156 us (26%)
  local copies, waits for them, and re-layouts  138 us (23%)
  other arithmetic  90 us (15%)
  starting transfers between devices  16 us (3%)
  between operations  14.2 us (2%)
    all_gather x1, blocking collectives, shards(): row_router = lax.all_gather(part_router, 'fsdp', axis=0, tiled=True)  131 us
    all_to_all x1, waiting for transfers between devices, shards(): lax.all_to_all(narrow_up, 'fsdp', split_axis=2, concat_axis=1, tiled=True)  95.7 us
    psum x1, waiting for transfers between devices, shards(): lax.psum(jnp.sum(jnp.abs(train_up), axis=1).astype(jnp.bfloat16), 'fsdp')  83.2 us
    unnamed x9, local copies, waits for them, and re-layouts  48.1 us
    convert_element_type x1, other arithmetic, shards(): (train_down / jnp.expand_dims(scale_down, 2)).astype(jnp.bfloat16)  32.6 us
    all_to_all x2, local copies, waits for them, and re-layouts, shards(): lax.all_to_all(narrow_down, 'fsdp', split_axis=1, concat_axis=2, tiled=True)  29.3 us
    all_to_all x2, local copies, waits for them, and re-layouts, shards(): lax.all_to_all(narrow_gate, 'fsdp', split_axis=2, concat_axis=1, tiled=True)  29.3 us
    all_to_all x2, local copies, waits for them, and re-layouts, shards(): lax.all_to_all(narrow_up, 'fsdp', split_axis=2, concat_axis=1, tiled=True)  29.3 us
  transfers between devices with their start and end apart: 4, of which 2 were waited for; matrix products, arithmetic and copies ran while one was open for 19% of the time, Pallas kernels for 0%

profile of v1, /device:TPU:0, one launch (start us, length us, event | category | flops | bytes accessed | tf_op | source)
XLA Modules:
  0.0 593.4 jit_solution(10521997771390271099)
XLA Ops:
  7.2 23.7 %copy.35 = f32[16,256,1408]{1,0,2:T(8,128)} copy(f32[16,256,1408]{2,1,0:T(8,128)} %param.5) | data formatting | bytes 46137344 | tf_op args[0]
  30.8 9.2 %abs_reduce_fusion.2 = bf16[16,1408]{1,0:T(8,128)(2,1)S(1)} fusion(f32[16,256,1408]{2,1,0:T(8,128)} %param.5), kind=kLoop, calls=%fused_computation.6 | loop fusion | flops 11511808 | bytes 23113728 | tf_op jit(solution)/shard_map/reduce_sum | solution.py:12
  40.1 11.1 %all-gather = bf16[128,1408]{1,0:T(8,128)(2,1)S(1)} all-gather(bf16[16,1408]{1,0:T(8,128)(2,1)S(1)} %abs_reduce_fusion.2), channel_id=2, replica_groups=mesh['ep'=4,'fsdp'=8] {'fsdp'}, dimensions={0}, use_global_device_ids=true | all-gather | bytes 405504 | tf_op jit(solution)/shard_map/all_gather | solution.py:12
  51.5 14.2 %divide_convert_fusion.1 = bf16[16,256,1408]{1,0,2:T(8,128)(2,1)} fusion(f32[16,256,1408]{1,0,2:T(8,128)} %copy.35, f32[16,1408]{0,1:T(8,128)S(1)} %copy.34), kind=kLoop, calls=%fused_computation.5 | loop fusion | flops 11534336 | bytes 34693120 | tf_op jit(solution)/shard_map/convert_element_type | solution.py:26
  65.7 5.2 all-to-all-start
  71.0 9.9 %abs_reduce_fusion.1 = bf16[16,1408]{1,0:T(8,128)(2,1)} fusion(f32[16,256,1408]{2,1,0:T(8,128)} %param.6), kind=kLoop, calls=%fused_computation.4 | loop fusion | flops 11511808 | bytes 23113728 | tf_op jit(solution)/shard_map/reduce_sum | solution.py:15
  80.9 9.0 %abs_reduce_fusion = bf16[16,1408]{1,0:T(8,128)(2,1)} fusion(f32[16,1408,256]{2,1,0:T(8,128)} %param.7), kind=kLoop, calls=%fused_computation.2 | loop fusion | flops 11511808 | bytes 23113728 | tf_op jit(solution)/shard_map/reduce_sum | solution.py:18
  89.9 23.7 %copy.39 = f32[16,256,1408]{1,0,2:T(8,128)} copy(f32[16,256,1408]{2,1,0:T(8,128)} %param.6) | data formatting | bytes 46137344 | tf_op args[1]
  113.6 83.2 %all-reduce.3.cloned.1.call-done = (bf16[16,1408]{1,0:T(8,128)(2,1)}, bf16[16,1408]{1,0:T(8,128)(2,1)}) async-done(((bf16[16,1408]{1,0:T(8,128)(2,1)}, bf16[16,1408]{1,0:T(8,128)(2,1)}), (bf16[16,1408]{1,0:T(8,128)(2,1)}, bf16[16,1408]{1,0:T(8,128)(2,1)})) %all-reduce.3.cloned.1.call-update) | async-done | bytes 90128 | tf_op jit(solution)/shard_map/psum | solution.py:15
  196.8 0.8 convert_multiply_fusion.1
  197.9 14.2 %divide_convert_fusion = bf16[16,256,1408]{1,0,2:T(8,128)(2,1)} fusion(f32[16,256,1408]{1,0,2:T(8,128)} %copy.39, f32[16,1408]{0,1:T(8,128)S(1)} %copy.38), kind=kLoop, calls=%fused_computation.3 | loop fusion | flops 11534336 | bytes 34693120 | tf_op jit(solution)/shard_map/convert_element_type | solution.py:27
  212.1 5.5 all-to-all-start.1
  217.9 32.6 %fusion = bf16[16,1408,256]{2,0,1:T(8,128)(2,1)} fusion(f32[16,1408,256]{2,1,0:T(8,128)} %param.7, f32[16,1408]{0,1:T(8,128)S(1)} %copy.42), kind=kLoop, calls=%fused_computation.1 | loop fusion | flops 11534336 | bytes 34693120 | tf_op jit(solution)/shard_map/convert_element_type | solution.py:28
  250.5 95.7 %all-to-all-done.1 = bf16[16,256,1408]{1,0,2:T(8,128)(2,1)} async-done(((bf16[16,256,1408]{1,0,2:T(8,128)(2,1)}), bf16[16,256,1408]{1,0,2:T(8,128)(2,1)}, u32[]{:S(2)}, u32[]{:S(2)}) %all-to-all-start.1) | async-done | bytes 11534368 | tf_op jit(solution)/shard_map/all_to_all | solution.py:32
  346.2 5.3 all-to-all-start.2
  351.5 130.9 %all_gather.11 = bf16[2048,16]{0,1:T(8,128)(2,1)S(1)} all-gather(bf16[256,16]{0,1:T(8,128)(2,1)S(1)} %multiply_convert_fusion), channel_id=1, replica_groups=mesh['ep'=4,'fsdp'=8] {'fsdp'}, dimensions={0}, use_global_device_ids=true | all-gather | bytes 73728 | tf_op jit(solution)/shard_map/all_gather | solution.py:45
  482.4 14.1 %all_gather.12 = bf16[2048,64]{0,1:T(8,128)(2,1)S(1)} all-gather(bf16[2048,16]{0,1:T(8,128)(2,1)S(1)} %all_gather.11), channel_id=1, replica_groups=mesh['ep'=4,'fsdp'=8] {'ep'}, dimensions={1}, use_global_device_ids=true | all-gather | bytes 327680 | tf_op jit(solution)/shard_map/all_gather | solution.py:46
  497.9 11.3 %copy.37 = bf16[16,8,256,176]{2,1,3,0:T(8,128)(2,1)} copy(bf16[16,8,256,176]{2,0,3,1:T(8,128)(2,1)} %bitcast.3) | data formatting | bytes 23068672 | tf_op jit(solution)/shard_map/all_to_all | solution.py:31
  509.2 18.0 %all_to_all.42 = bf16[16,2048,176]{1,2,0:T(8,128)(2,1)} reshape(bf16[16,8,256,176]{2,1,3,0:T(8,128)(2,1)} %copy.37) | data formatting | bytes 23068672 | tf_op jit(solution)/shard_map/all_to_all | solution.py:31
  527.2 11.3 %copy.41 = bf16[16,8,256,176]{2,1,3,0:T(8,128)(2,1)} copy(bf16[16,8,256,176]{2,0,3,1:T(8,128)(2,1)} %bitcast.6) | data formatting | bytes 23068672 | tf_op jit(solution)/shard_map/all_to_all | solution.py:32
  538.5 18.0 %all_to_all.46 = bf16[16,2048,176]{1,2,0:T(8,128)(2,1)} reshape(bf16[16,8,256,176]{2,1,3,0:T(8,128)(2,1)} %copy.41) | data formatting | bytes 23068672 | tf_op jit(solution)/shard_map/all_to_all | solution.py:32
  556.5 11.4 %copy.44 = bf16[16,176,8,256]{3,2,1,0:T(8,128)(2,1)} copy(bf16[16,176,8,256]{3,0,1,2:T(8,128)(2,1)} %bitcast.8) | data formatting | bytes 23068672 | tf_op jit(solution)/shard_map/all_to_all | solution.py:34
  567.8 18.0 %all_to_all.50 = bf16[16,176,2048]{2,1,0:T(8,128)(2,1)} reshape(bf16[16,176,8,256]{3,2,1,0:T(8,128)(2,1)} %copy.44) | data formatting | bytes 23068672 | tf_op jit(solution)/shard_map/all_to_all | solution.py:34
  585.8 0.7 copy.53
  (19 shorter events, 2.3 us)
Async XLA Ops:
  65.7 146.4 %all-to-all-start = ((bf16[16,256,1408]{1,0,2:T(8,128)(2,1)}), bf16[16,256,1408]{1,0,2:T(8,128)(2,1)}, u32[]{:S(2)}, u32[]{:S(2)}) async-start(bf16[16,256,1408]{1,0,2:T(8,128)(2,1)} %divide_convert_fusion.1), calls=%async_computation | async-start | bytes 23068672 | tf_op jit(solution)/shard_map/all_to_all | solution.py:31
  71.0 125.9 %all-reduce.3.cloned.1.call-start = ((), (), s32[]{:S(2)}) async-start(), calls=%async_computation.3 | async-start | bytes 180224 | tf_op jit(solution)/shard_map/psum | solution.py:15
  197.9 19.7 %copy-start = (bf16[16,1408]{1,0:T(8,128)(2,1)S(1)}, bf16[16,1408]{1,0:T(8,128)(2,1)}, u32[]{:S(2)}) copy-start(bf16[16,1408]{1,0:T(8,128)(2,1)} %get-tuple-element.8) | copy-start | bytes 135172
  212.1 134.1 %all-to-all-start.1 = ((bf16[16,256,1408]{1,0,2:T(8,128)(2,1)}), bf16[16,256,1408]{1,0,2:T(8,128)(2,1)}, u32[]{:S(2)}, u32[]{:S(2)}) async-start(bf16[16,256,1408]{1,0,2:T(8,128)(2,1)} %divide_convert_fusion), calls=%async_computation.1 | async-start | bytes 23068672 | tf_op jit(solution)/shard_map/all_to_all | solution.py:32
  217.9 133.6 %copy-start.1 = (f32[256,16]{0,1:T(8,128)S(1)}, f32[256,16]{0,1:T(8,128)}, u32[]{:S(2)}) copy-start(f32[256,16]{0,1:T(8,128)} %param.8) | copy-start | bytes 49156
  217.9 133.6 %copy-start.2 = (f32[256]{0:T(256)S(1)}, f32[256]{0:T(256)}, u32[]{:S(2)}) copy-start(f32[256]{0:T(256)} %param.9) | copy-start | bytes 3076
  346.2 210.3 %all-to-all-start.2 = ((bf16[16,1408,256]{2,0,1:T(8,128)(2,1)}), bf16[16,1408,256]{2,0,1:T(8,128)(2,1)}, u32[]{:S(2)}, u32[]{:S(2)}) async-start(bf16[16,1408,256]{2,0,1:T(8,128)(2,1)} %fusion), calls=%async_computation.2 | async-start | bytes 23068672 | tf_op jit(solution)/shard_map/all_to_all | solution.py:34
Sparse Core Ops, SparseCore 0:
  90.0 106.7 all-reduce.2
